TPU v7x, 256 devices: a whole 4x4x8 slice. The times are simulated.
256 devices in a mesh: rep: 4 (over z_hi), exp: 64 (over z_lo, x, y, core).
Axes of the slice: x: 4, y: 4, z: 8 (z_hi: 4, z_lo: 2; z = z_hi * 2 + z_lo), core: 2. Of those that a mesh axis runs over, the one named last changes fastest.
Arguments:
- act_a: bfloat16 [32768, 3584], P(('rep', 'exp')), may hold values from -6 to 6
- grad_a: bfloat16 [32768, 2, 1024], P(('rep', 'exp')), may hold values from -0.125 to 0.125
- route_a: int32 [32768, 2], P(('rep', 'exp')), may hold values from 0 to 63, all different within a row; in each aligned block of 128 rows (0 to 127, 128 to 255, ...) at most 5 rows name the same one
- act_b: bfloat16 [32768, 3584], P(('rep', 'exp')), may hold values from -6 to 6
- grad_b: bfloat16 [32768, 2, 1024], P(('rep', 'exp')), may hold values from -0.125 to 0.125
- route_b: int32 [32768, 2], P(('rep', 'exp')), may hold values from 0 to 31, all different within a row; in each aligned block of 128 rows (0 to 127, 128 to 255, ...) at most 10 rows name the same one
Outputs:
- wgrad_a: bfloat16 [64, 3584, 1024], P('exp', 'rep')
- wgrad_b: bfloat16 [64, 1792, 1024], P('exp', 'rep')
Inputs may be any that keep to these rules, and one draw needn't show every extreme that they name: `route_a`: each token names 2 different experts of layer A; the 128 tokens of one device name any one expert at most 5 times. `route_b`: each token names 2 different experts of layer B; the 128 tokens of one device name any one expert at most 2 * 5 times.
All inputs are finite; a program needn't handle non-finite values.
Results may differ from a plain program's by a relative error of at most 0.013.
Values may be sent and summed in bfloat16 or wider, within the bound.
No kernel may reach another device: no remote copies, remote signals or barrier semaphores. Data moves between devices by JAX's collectives and lax.ppermute only.
A program may use at most 128 MiB of HBM per device.

v0:
```python
import jax
import jax.numpy as jnp
from jax import lax
from jax.sharding import PartitionSpec as P


def sent_together(arrays, axis, split_dim, concat_dim, along):
    ends, at = ([], 0)
    for a in arrays[:-1]:
        at += a.shape[along]
        ends.append(at)
    both = jnp.concatenate(arrays, axis=along)
    return tuple(
        jnp.split(
            lax.all_to_all(both, axis, split_axis=split_dim, concat_axis=concat_dim, tiled=True),
            ends,
            axis=along,
        )
    )


def sent_to_all(array, axis):
    size = lax.axis_size(axis)
    return lax.all_to_all(
        jnp.broadcast_to(array[None], (size, *array.shape)), axis, 0, 0, tiled=True
    )


def joined_along(parts, dim):
    parts = jnp.moveaxis(parts, 0, dim)
    dims = parts.shape
    return parts.reshape(*dims[:dim], dims[dim] * dims[dim + 1], *dims[dim + 2 :])


def gather_directly(array, axis, dim):
    parts = sent_to_all(array, axis)
    return joined_along(parts, dim)


def from_partner(block, axis, apart):
    count = lax.axis_size(axis)
    route = []
    for low in range(count):
        high = low | 1 << apart
        if high != low and high < count:
            route += [(low, high), (high, low)]
    return lax.ppermute(block, axis, route)


def slot_sources(route, experts, stride, slot_count):
    flat_ids = route.reshape(-1)
    onehot = (flat_ids[:, None] == jnp.arange(experts, dtype=jnp.int32)[None, :]).astype(jnp.int32)
    before = jnp.cumsum(onehot, axis=0) - onehot
    position = jnp.sum(before * onehot, axis=1)
    slot_index = flat_ids * stride + position
    pair_ids = jnp.arange(flat_ids.shape[0], dtype=jnp.int32)
    return jnp.full((slot_count,), -1, jnp.int32).at[slot_index].set(pair_ids)


def fill_rows(acts, grads, sources, top_count):
    filled = (sources >= 0)[:, None]
    clamped = jnp.maximum(sources, 0)
    rows_act = jnp.where(filled, acts[clamped // top_count], jnp.zeros((), acts.dtype))
    flat_grads = grads.reshape(-1, grads.shape[-1])
    rows_grad = jnp.where(filled, flat_grads[clamped], jnp.zeros((), grads.dtype))
    return (rows_act, rows_grad)


def contract(left, right):
    return lax.dot_general(
        left, right, (((0,), (0,)), ((), ())), preferred_element_type=jnp.float32
    )


def shards(act_a, grad_a, route_a, act_b, grad_b, route_b):
    exp_count = lax.axis_size("exp")
    token_count = act_a.shape[0]
    top_count = route_a.shape[1]
    features = act_a.shape[1]
    hidden = grad_a.shape[2]
    most_rows = token_count * top_count * 5 // (4 * exp_count)
    sources_a = slot_sources(route_a, exp_count, most_rows, exp_count * most_rows)
    send_act, send_grad = fill_rows(act_a, grad_a, sources_a, top_count)
    recv_act, recv_grad = sent_together((send_act, send_grad), "exp", 0, 0, 1)
    columns_mine = lax.all_to_all(recv_act, "rep", split_axis=1, concat_axis=0, tiled=True)
    owned_a = contract(columns_mine, gather_directly(recv_grad, "rep", 0))
    wgrad_a = owned_a.astype(jnp.bfloat16)[None]
    half_exp = exp_count // 2
    sources_b = slot_sources(route_b, half_exp, 2 * most_rows, exp_count * most_rows)
    send_act_b, send_grad_b = fill_rows(act_b, grad_b, sources_b, top_count)
    recv_act_b, recv_grad_b = sent_together((send_act_b, send_grad_b), "exp", 0, 0, 1)
    partial_value = (
        contract(recv_act_b, recv_grad_b).astype(jnp.bfloat16).reshape(2, features // 2, hidden)
    )
    parity = lax.axis_index("exp") % 2
    kept_half = lax.dynamic_index_in_dim(partial_value, parity, 0, keepdims=False)
    sent_half = lax.dynamic_index_in_dim(partial_value, 1 - parity, 0, keepdims=False)
    arrived = from_partner(sent_half, "exp", 0)
    paired = (kept_half.astype(jnp.float32) + arrived.astype(jnp.float32)).astype(jnp.bfloat16)
    owned_b = lax.psum_scatter(paired, "rep", scatter_dimension=0, tiled=True).astype(jnp.float32)
    wgrad_b = owned_b.astype(jnp.bfloat16)[None]
    return (wgrad_a, wgrad_b)


def solution(mesh):
    return jax.shard_map(
        shards,
        mesh=mesh,
        in_specs=(
            P(("rep", "exp"), None),
            P(("rep", "exp"), None, None),
            P(("rep", "exp"), None),
            P(("rep", "exp"), None),
            P(("rep", "exp"), None, None),
            P(("rep", "exp"), None),
        ),
        out_specs=(P("exp", "rep", None), P("exp", "rep", None)),
        check_vma=False,
    )
```

profile of v0, /device:TPU:34, one launch (start us, length us, event | category | flops | bytes accessed | tf_op | source)
XLA Modules:
  0.0 382.3 jit_solution(356382941867029190)
XLA Ops:
  7.2 0.9 copy.14
  8.2 0.1 eq.60
  8.3 0.7 broadcast_multiply_fusion
  9.0 0.6 reduce-window.16
  9.6 0.2 slice_reduce_fusion.1
  10.0 0.1 mul.44
  10.2 1.4 scatter_custom_fusion.1
  11.7 3.1 gather_fusion.2
  14.8 2.7 gather.25
  17.5 0.1 broadcast_in_dim.79
  17.6 1.2 reshape.147
  18.9 2.1 gather_fusion.3
  21.0 0.3 gather.27
  21.3 2.4 broadcast_select_fusion
  23.7 0.2 broadcast_select_fusion.2
  23.9 3.0 pad_maximum_fusion.1
  26.9 9.4 %all-to-all-start.3 = ((bf16[64,5,4608]{2,1,0:T(8,128)(2,1)}), bf16[64,5,4608]{2,1,0:T(8,128)(2,1)}, u32[]{:S(2)}, u32[]{:S(2)}) async-start(bf16[64,5,4608]{2,1,0:T(8,128)(2,1)} %pad_maximum_fusion.1), calls=%async_computation.3 | async-start | bytes 9437184 | tf_op jit(solution)/shard_map/all_to_all | solution.py:15
  36.4 0.1 eq.56
  36.5 0.1 eq.52
  36.7 0.6 reduce-window.14
  37.3 0.2 slice_reduce_fusion
  37.6 0.1 mul.40
  37.9 1.6 scatter_custom_fusion
  39.5 3.1 gather_fusion
  42.7 2.7 gather.21
  45.4 0.1 broadcast_in_dim.70
  45.5 1.2 reshape.145
  46.8 2.1 gather_fusion.1
  48.9 0.3 gather.23
  49.1 0.2 broadcast_select_fusion.3
  49.3 2.4 broadcast_select_fusion.1
  51.7 3.0 pad_maximum_fusion
  54.7 40.7 %all-to-all-done.3 = bf16[64,5,4608]{2,1,0:T(8,128)(2,1)} async-done(((bf16[64,5,4608]{2,1,0:T(8,128)(2,1)}), bf16[64,5,4608]{2,1,0:T(8,128)(2,1)}, u32[]{:S(2)}, u32[]{:S(2)}) %all-to-all-start.3) | async-done | bytes 2949152 | tf_op jit(solution)/shard_map/all_to_all | solution.py:15
  95.4 8.5 %all-to-all-start = ((bf16[64,5,4608]{2,1,0:T(8,128)(2,1)}), bf16[64,5,4608]{2,1,0:T(8,128)(2,1)}, u32[]{:S(2)}, u32[]{:S(2)}) async-start(bf16[64,5,4608]{2,1,0:T(8,128)(2,1)} %pad_maximum_fusion), calls=%async_computation | async-start | bytes 9437184 | tf_op jit(solution)/shard_map/all_to_all | solution.py:15
  103.9 5.1 %all_to_all.34 = bf16[320,4608]{1,0:T(8,128)(2,1)} reshape(bf16[64,5,4608]{2,1,0:T(8,128)(2,1)} %all-to-all-done.3) | data formatting | bytes 5898240 | tf_op jit(solution)/shard_map/all_to_all | solution.py:15
  108.9 5.8 %convolution_convert_fusion = bf16[3584,1024]{1,0:T(8,128)(2,1)S(1)} fusion(bf16[320,4608]{1,0:T(8,128)(2,1)} %all_to_all.34), kind=kOutput, calls=%fused_computation.6 | convolution fusion | flops 2352480256 | bytes 10289152 | tf_op jit(solution)/shard_map/dot_general | solution.py:70
  114.7 2.5 dynamic-slice_bitcast_fusion
  117.2 1.7 copy-done.3
  119.0 43.9 %all-to-all-done = bf16[64,5,4608]{2,1,0:T(8,128)(2,1)} async-done(((bf16[64,5,4608]{2,1,0:T(8,128)(2,1)}), bf16[64,5,4608]{2,1,0:T(8,128)(2,1)}, u32[]{:S(2)}, u32[]{:S(2)}) %all-to-all-start) | async-done | bytes 2949152 | tf_op jit(solution)/shard_map/all_to_all | solution.py:15
  163.0 5.0 %all_to_all.28 = bf16[320,4608]{1,0:T(8,128)(2,1)} reshape(bf16[64,5,4608]{2,1,0:T(8,128)(2,1)} %all-to-all-done) | data formatting | bytes 5898240 | tf_op jit(solution)/shard_map/all_to_all | solution.py:15
  168.0 1.6 slice-done
  169.6 1.6 copy.23
  171.3 7.6 %all-to-all-start.1 = ((bf16[320,4,896]{2,0,1:T(8,128)(2,1)}), bf16[320,4,896]{2,0,1:T(8,128)(2,1)S(1)}, u32[]{:S(2)}, u32[]{:S(2)}) async-start(bf16[320,4,896]{2,0,1:T(8,128)(2,1)} %bitcast.66), calls=%async_computation.1 | async-start | bytes 4587520 | tf_op jit(solution)/shard_map/all_to_all | solution.py:85
  178.8 6.9 %fusion = bf16[1792,1024]{1,0:T(8,128)(2,1)} fusion(bf16[1792,1024]{1,0:T(8,128)(2,1)} %collective-permute-done, bf16[2,1792,1024]{2,1,0:T(8,128)(2,1)} %bitcast.68, s32[]{:T(128)S(6)} %select_n.79), kind=kLoop, calls=%fused_computation.8 | loop fusion | flops 7340032 | bytes 11010052 | tf_op jit(solution)/shard_map/convert_element_type | solution.py:99
  185.8 130.6 %all-to-all-done.1 = bf16[320,4,896]{2,0,1:T(8,128)(2,1)S(1)} async-done(((bf16[320,4,896]{2,0,1:T(8,128)(2,1)}), bf16[320,4,896]{2,0,1:T(8,128)(2,1)S(1)}, u32[]{:S(2)}, u32[]{:S(2)}) %all-to-all-start.1) | async-done | bytes 2293792 | tf_op jit(solution)/shard_map/all_to_all | solution.py:85
  316.3 0.3 broadcast_in_dim.77
  316.6 55.0 %all_to_all.39 = bf16[4,320,1024]{2,1,0:T(8,128)(2,1)S(1)} all-to-all(bf16[4,320,1024]{2,1,0:T(8,128)(2,1)S(1)} %broadcast_in_dim.77), channel_id=1, replica_groups=mesh['rep'=4,'exp'=64] {'rep'}, dimensions={0} | all-to-all | bytes 5242880 | tf_op jit(solution)/shard_map/all_to_all | solution.py:24
  371.7 3.8 %fusion.4 = bf16[1,896,1024]{2,1,0:T(8,128)(2,1)} fusion(bf16[4,320,1024]{2,1,0:T(8,128)(2,1)S(1)} %all_to_all.39, bf16[320,4,896]{2,0,1:T(8,128)(2,1)S(1)} %all-to-all-done.1), kind=kOutput, calls=%fused_computation.19 | convolution fusion | flops 2349727744 | bytes 6750208 | tf_op jit(solution)/shard_map/dot_general | solution.py:70
  (40 shorter events, 1.0 us)
Async XLA Ops:
  7.2 4.5 %copy-start = (bf16[128,3584]{1,0:T(8,128)(2,1)S(1)}, bf16[128,3584]{1,0:T(8,128)(2,1)}, u32[]{:S(2)}) copy-start(bf16[128,3584]{1,0:T(8,128)(2,1)} %param.9) | copy-start | bytes 2752516
  26.9 9.4 %copy-start.4 = (s32[128,2]{0,1:T(2,128)S(1)}, s32[128,2]{0,1:T(2,128)}, u32[]{:S(2)}) copy-start(s32[128,2]{0,1:T(2,128)} %param.8) | copy-start | bytes 3076
  26.9 12.7 %copy-start.2 = (bf16[128,3584]{1,0:T(8,128)(2,1)S(1)}, bf16[128,3584]{1,0:T(8,128)(2,1)}, u32[]{:S(2)}) copy-start(bf16[128,3584]{1,0:T(8,128)(2,1)} %param.6) | copy-start | bytes 2752516
  26.9 68.5 %all-to-all-start.3 = ((bf16[64,5,4608]{2,1,0:T(8,128)(2,1)}), bf16[64,5,4608]{2,1,0:T(8,128)(2,1)}, u32[]{:S(2)}, u32[]{:S(2)}) async-start(bf16[64,5,4608]{2,1,0:T(8,128)(2,1)} %pad_maximum_fusion.1), calls=%async_computation.3 | async-start | bytes 9437184 | tf_op jit(solution)/shard_map/all_to_all | solution.py:15
  95.4 67.6 %all-to-all-start = ((bf16[64,5,4608]{2,1,0:T(8,128)(2,1)}), bf16[64,5,4608]{2,1,0:T(8,128)(2,1)}, u32[]{:S(2)}, u32[]{:S(2)}) async-start(bf16[64,5,4608]{2,1,0:T(8,128)(2,1)} %pad_maximum_fusion), calls=%async_computation | async-start | bytes 9437184 | tf_op jit(solution)/shard_map/all_to_all | solution.py:15
  114.7 4.2 %copy-start.3 = (bf16[3584,1024]{1,0:T(8,128)(2,1)}, bf16[3584,1024]{1,0:T(8,128)(2,1)S(1)}, u32[]{:S(2)}) copy-start(bf16[3584,1024]{1,0:T(8,128)(2,1)S(1)} %convolution_convert_fusion) | copy-start | bytes 22020100
  118.9 59.9 %collective-permute-start = (bf16[1792,1024]{1,0:T(8,128)(2,1)}, bf16[1792,1024]{1,0:T(8,128)(2,1)}, u32[]{:S(2)}, u32[]{:S(2)}) collective-permute-start(bf16[1792,1024]{1,0:T(8,128)(2,1)} %dynamic-slice_bitcast_fusion), channel_id=1, source_target_pairs={{0,1},{1,0},{2,3},{3,2},{4,5},{5,4},{6,7},{7,6},{8,9},{9,8},{10,11... | collective-permute-start | bytes 11010056 | tf_op jit(solution)/shard_map/ppermute | solution.py:47
  168.0 1.6 slice-start
  171.3 145.0 %all-to-all-start.1 = ((bf16[320,4,896]{2,0,1:T(8,128)(2,1)}), bf16[320,4,896]{2,0,1:T(8,128)(2,1)S(1)}, u32[]{:S(2)}, u32[]{:S(2)}) async-start(bf16[320,4,896]{2,0,1:T(8,128)(2,1)} %bitcast.66), calls=%async_computation.1 | async-start | bytes 4587520 | tf_op jit(solution)/shard_map/all_to_all | solution.py:85
  178.8 196.7 %reduce-scatter.2.cloned.1.call-start = ((), (), s32[]{:S(2)}) async-start(), calls=%async_computation.5 | async-start | bytes 4587520 | tf_op jit(solution)/shard_map/reduce_scatter | solution.py:100
  185.7 130.6 %slice-start.1 = ((bf16[320,4608]{1,0:T(8,128)(2,1)}), bf16[320,1024]{1,0:T(8,128)(2,1)S(1)}, s32[]{:S(2)}) async-start(bf16[320,4608]{1,0:T(8,128)(2,1)} %all_to_all.28), calls=%async_computation.7 | async-start | bytes 1310720 | tf_op jit(solution)/shard_map/split | solution.py:14
  371.7 3.8 %copy-start.1 = (bf16[128,3584]{1,0:T(8,128)(2,1)S(1)}, bf16[128,3584]{1,0:T(8,128)(2,1)}, u32[]{:S(2)}) copy-start(bf16[128,3584]{1,0:T(8,128)(2,1)} %param.9) | copy-start | bytes 2752516
Sparse Core Ops, SparseCore 0:
  185.9 157.8 reduce-scatter.1
where the time goes:
time: 383 us; the launch traced here: 382 us
  waiting for transfers between devices  215 us (56%)
  blocking collectives  55 us (14%)
  local copies, waits for them, and re-layouts  42.4 us (11%)
  starting transfers between devices  25.5 us (7%)
  other arithmetic  20.3 us (5%)
  between operations  14.3 us (4%)
  matrix products  9.63 us (3%)
    all_to_all x1, waiting for transfers between devices, shards(): lax.all_to_all(recv_act, 'rep', split_axis=1, concat_axis=0, tiled=True)  131 us
    all_to_all x2, waiting for transfers between devices, sent_together(): lax.all_to_all(both, axis, split_axis=split_dim, concat_axis=concat_dim,...  84.6 us
    all_to_all x1, blocking collectives, sent_to_all(): lax.all_to_all(jnp.broadcast_to(array[None], (size, *array.shape)), axis,...  55 us
    all_to_all x2, starting transfers between devices, sent_together(): lax.all_to_all(both, axis, split_axis=split_dim, concat_axis=concat_dim,...  17.8 us
    gather x4, local copies, waits for them, and re-layouts, fill_rows(): acts[clamped // top_count]  11.6 us
    all_to_all x2, local copies, waits for them, and re-layouts, sent_together(): lax.all_to_all(both, axis, split_axis=split_dim, concat_axis=concat_dim,...  10.1 us
    dot_general x2, matrix products, contract(): lax.dot_general(left, right, (((0,), (0,)), ((), ())), preferred_element_...  9.63 us
  transfers between devices with their start and end apart: 5, of which 3 were waited for; matrix products, arithmetic and copies ran while one was open for 10% of the time, Pallas kernels for 0%

commit v1 on v0

--- a/solution.py
+++ b/solution.py
@@ -2,6 +2,7 @@
 import jax.numpy as jnp
 from jax import lax
 from jax.sharding import PartitionSpec as P
+from jax.lax import all_to_all, axis_size
 
 
 def sent_together(arrays, axis, split_dim, concat_dim, along):
@@ -82,7 +83,10 @@
     sources_a = slot_sources(route_a, exp_count, most_rows, exp_count * most_rows)
     send_act, send_grad = fill_rows(act_a, grad_a, sources_a, top_count)
     recv_act, recv_grad = sent_together((send_act, send_grad), "exp", 0, 0, 1)
-    columns_mine = lax.all_to_all(recv_act, "rep", split_axis=1, concat_axis=0, tiled=True)
+    v1 = axis_size("rep")
+    mixed_arr = jnp.split(recv_act, v1, axis=1)
+    earlier = jnp.stack(mixed_arr)
+    columns_mine = jnp.concatenate(all_to_all(earlier, "rep", 0, 0), axis=0)
     owned_a = contract(columns_mine, gather_directly(recv_grad, "rep", 0))
     wgrad_a = owned_a.astype(jnp.bfloat16)[None]
     half_exp = exp_count // 2

time: 383 us -> 383 us (level)
  transfers between devices with their start and end apart: 5 -> 5, of which waited for: 3 -> 3; matrix products, arithmetic and copies ran while one was open for 10% -> 11% of each run, Pallas kernels for 0% -> 0%
where the time goes in v1:
time: 383 us
  waiting for transfers between devices  215 us (56%)
  blocking collectives  55 us (14%)
  local copies, waits for them, and re-layouts  40.9 us (11%)
  starting transfers between devices  25.5 us (7%)
  other arithmetic  22.1 us (6%)
  between operations  14.3 us (4%)
  matrix products  9.62 us (3%)
    all_to_all x1, waiting for transfers between devices, shards(): columns_mine = jnp.concatenate(all_to_all(earlier, 'rep', 0, 0), axis=0)  131 us
    all_to_all x2, waiting for transfers between devices, sent_together(): lax.all_to_all(both, axis, split_axis=split_dim, concat_axis=concat_dim,...  84.6 us
    all_to_all x1, blocking collectives, sent_to_all(): lax.all_to_all(jnp.broadcast_to(array[None], (size, *array.shape)), axis,...  55 us
    all_to_all x2, starting transfers between devices, sent_together(): lax.all_to_all(both, axis, split_axis=split_dim, concat_axis=concat_dim,...  17.8 us
    gather x4, local copies, waits for them, and re-layouts, fill_rows(): acts[clamped // top_count]  11.6 us
    all_to_all x2, local copies, waits for them, and re-layouts, sent_together(): lax.all_to_all(both, axis, split_axis=split_dim, concat_axis=concat_dim,...  10.1 us
    dot_general x2, matrix products, contract(): lax.dot_general(left, right, (((0,), (0,)), ((), ())), preferred_element_...  9.62 us
  transfers between devices with their start and end apart: 5, of which 3 were waited for; matrix products, arithmetic and copies ran while one was open for 11% of the time, Pallas kernels for 0%

profile of v1, /device:TPU:34, one launch (start us, length us, event | category | flops | bytes accessed | tf_op | source)
XLA Modules:
  0.0 382.6 jit_solution(11966342506521808380)
XLA Ops:
  7.2 0.9 copy.13
  8.2 0.1 eq.60
  8.3 0.7 broadcast_multiply_fusion
  9.0 0.6 reduce-window.16
  9.6 0.2 slice_reduce_fusion.1
  10.0 0.1 mul.44
  10.2 1.4 scatter_custom_fusion.1
  11.7 3.1 gather_fusion.2
  14.8 2.7 gather.25
  17.5 0.1 broadcast_in_dim.79
  17.6 1.2 reshape.145
  18.9 2.1 gather_fusion.3
  21.0 0.3 gather.27
  21.3 2.4 broadcast_select_fusion
  23.7 0.2 broadcast_select_fusion.2
  23.9 3.0 pad_maximum_fusion.1
  26.9 9.4 %all-to-all-start.3 = ((bf16[64,5,4608]{2,1,0:T(8,128)(2,1)}), bf16[64,5,4608]{2,1,0:T(8,128)(2,1)}, u32[]{:S(2)}, u32[]{:S(2)}) async-start(bf16[64,5,4608]{2,1,0:T(8,128)(2,1)} %pad_maximum_fusion.1), calls=%async_computation.3 | async-start | bytes 9437184 | tf_op jit(solution)/shard_map/all_to_all | solution.py:16
  36.4 0.1 eq.56
  36.5 0.1 eq.52
  36.7 0.6 reduce-window.14
  37.3 0.2 slice_reduce_fusion
  37.6 0.1 mul.40
  37.9 1.6 scatter_custom_fusion
  39.5 3.1 gather_fusion
  42.7 2.7 gather.21
  45.4 0.1 broadcast_in_dim.70
  45.5 1.2 reshape.143
  46.8 2.1 gather_fusion.1
  48.9 0.3 gather.23
  49.1 0.2 broadcast_select_fusion.3
  49.3 2.4 broadcast_select_fusion.1
  51.7 3.0 pad_maximum_fusion
  54.7 40.7 %all-to-all-done.3 = bf16[64,5,4608]{2,1,0:T(8,128)(2,1)} async-done(((bf16[64,5,4608]{2,1,0:T(8,128)(2,1)}), bf16[64,5,4608]{2,1,0:T(8,128)(2,1)}, u32[]{:S(2)}, u32[]{:S(2)}) %all-to-all-start.3) | async-done | bytes 2949152 | tf_op jit(solution)/shard_map/all_to_all | solution.py:16
  95.4 8.5 %all-to-all-start = ((bf16[64,5,4608]{2,1,0:T(8,128)(2,1)}), bf16[64,5,4608]{2,1,0:T(8,128)(2,1)}, u32[]{:S(2)}, u32[]{:S(2)}) async-start(bf16[64,5,4608]{2,1,0:T(8,128)(2,1)} %pad_maximum_fusion), calls=%async_computation | async-start | bytes 9437184 | tf_op jit(solution)/shard_map/all_to_all | solution.py:16
  103.9 5.1 %all_to_all.23 = bf16[320,4608]{1,0:T(8,128)(2,1)} reshape(bf16[64,5,4608]{2,1,0:T(8,128)(2,1)} %all-to-all-done.3) | data formatting | bytes 5898240 | tf_op jit(solution)/shard_map/all_to_all | solution.py:16
  108.9 5.8 %convolution_convert_fusion = bf16[3584,1024]{1,0:T(8,128)(2,1)S(1)} fusion(bf16[320,4608]{1,0:T(8,128)(2,1)} %all_to_all.23), kind=kOutput, calls=%fused_computation.6 | convolution fusion | flops 2352480256 | bytes 10289152 | tf_op jit(solution)/shard_map/dot_general | solution.py:71
  114.7 2.5 dynamic-slice_bitcast_fusion
  117.2 1.7 copy-done.3
  119.0 43.9 %all-to-all-done = bf16[64,5,4608]{2,1,0:T(8,128)(2,1)} async-done(((bf16[64,5,4608]{2,1,0:T(8,128)(2,1)}), bf16[64,5,4608]{2,1,0:T(8,128)(2,1)}, u32[]{:S(2)}, u32[]{:S(2)}) %all-to-all-start) | async-done | bytes 2949152 | tf_op jit(solution)/shard_map/all_to_all | solution.py:16
  163.0 5.0 %all_to_all.19 = bf16[320,4608]{1,0:T(8,128)(2,1)} reshape(bf16[64,5,4608]{2,1,0:T(8,128)(2,1)} %all-to-all-done) | data formatting | bytes 5898240 | tf_op jit(solution)/shard_map/all_to_all | solution.py:16
  168.0 1.8 slice_bitcast_fusion.3
  169.7 1.8 pad_maximum_fusion.2
  171.5 7.6 %all-to-all-start.1 = ((bf16[4,320,896]{2,1,0:T(8,128)(2,1)}), bf16[4,320,896]{2,1,0:T(8,128)(2,1)S(1)}, u32[]{:S(2)}, u32[]{:S(2)}) async-start(bf16[4,320,896]{2,1,0:T(8,128)(2,1)} %pad_maximum_fusion.2), calls=%async_computation.1 | async-start | bytes 4587520 | tf_op jit(solution)/shard_map/all_to_all | solution.py:89
  179.1 6.9 %fusion = bf16[1792,1024]{1,0:T(8,128)(2,1)} fusion(bf16[1792,1024]{1,0:T(8,128)(2,1)} %collective-permute-done, bf16[2,1792,1024]{2,1,0:T(8,128)(2,1)} %bitcast.66, s32[]{:T(128)S(6)} %select_n.79), kind=kLoop, calls=%fused_computation.8 | loop fusion | flops 7340032 | bytes 11010052 | tf_op jit(solution)/shard_map/convert_element_type | solution.py:103
  186.0 130.6 %all-to-all-done.1 = bf16[4,320,896]{2,1,0:T(8,128)(2,1)S(1)} async-done(((bf16[4,320,896]{2,1,0:T(8,128)(2,1)}), bf16[4,320,896]{2,1,0:T(8,128)(2,1)S(1)}, u32[]{:S(2)}, u32[]{:S(2)}) %all-to-all-start.1) | async-done | bytes 2293792 | tf_op jit(solution)/shard_map/all_to_all | solution.py:89
  316.6 0.3 broadcast_in_dim.77
  316.9 55.0 %all_to_all.28 = bf16[4,320,1024]{2,1,0:T(8,128)(2,1)S(1)} all-to-all(bf16[4,320,1024]{2,1,0:T(8,128)(2,1)S(1)} %broadcast_in_dim.77), channel_id=1, replica_groups=mesh['rep'=4,'exp'=64] {'rep'}, dimensions={0} | all-to-all | bytes 5242880 | tf_op jit(solution)/shard_map/all_to_all | solution.py:25
  371.9 3.8 %fusion.2 = bf16[1,896,1024]{2,1,0:T(8,128)(2,1)} fusion(bf16[4,320,896]{2,1,0:T(8,128)(2,1)S(1)} %all-to-all-done.1, bf16[4,320,1024]{2,1,0:T(8,128)(2,1)S(1)} %all_to_all.28), kind=kOutput, calls=%fused_computation.17 | convolution fusion | flops 2349727744 | bytes 6750208 | tf_op jit(solution)/shard_map/dot_general | solution.py:71
  (39 shorter events, 1.0 us)
Async XLA Ops:
  7.2 4.5 %copy-start = (bf16[128,3584]{1,0:T(8,128)(2,1)S(1)}, bf16[128,3584]{1,0:T(8,128)(2,1)}, u32[]{:S(2)}) copy-start(bf16[128,3584]{1,0:T(8,128)(2,1)} %param.9) | copy-start | bytes 2752516
  26.9 9.4 %copy-start.4 = (s32[128,2]{0,1:T(2,128)S(1)}, s32[128,2]{0,1:T(2,128)}, u32[]{:S(2)}) copy-start(s32[128,2]{0,1:T(2,128)} %param.8) | copy-start | bytes 3076
  26.9 12.7 %copy-start.2 = (bf16[128,3584]{1,0:T(8,128)(2,1)S(1)}, bf16[128,3584]{1,0:T(8,128)(2,1)}, u32[]{:S(2)}) copy-start(bf16[128,3584]{1,0:T(8,128)(2,1)} %param.6) | copy-start | bytes 2752516
  26.9 68.5 %all-to-all-start.3 = ((bf16[64,5,4608]{2,1,0:T(8,128)(2,1)}), bf16[64,5,4608]{2,1,0:T(8,128)(2,1)}, u32[]{:S(2)}, u32[]{:S(2)}) async-start(bf16[64,5,4608]{2,1,0:T(8,128)(2,1)} %pad_maximum_fusion.1), calls=%async_computation.3 | async-start | bytes 9437184 | tf_op jit(solution)/shard_map/all_to_all | solution.py:16
  95.4 67.6 %all-to-all-start = ((bf16[64,5,4608]{2,1,0:T(8,128)(2,1)}), bf16[64,5,4608]{2,1,0:T(8,128)(2,1)}, u32[]{:S(2)}, u32[]{:S(2)}) async-start(bf16[64,5,4608]{2,1,0:T(8,128)(2,1)} %pad_maximum_fusion), calls=%async_computation | async-start | bytes 9437184 | tf_op jit(solution)/shard_map/all_to_all | solution.py:16
  114.7 4.2 %copy-start.3 = (bf16[3584,1024]{1,0:T(8,128)(2,1)}, bf16[3584,1024]{1,0:T(8,128)(2,1)S(1)}, u32[]{:S(2)}) copy-start(bf16[3584,1024]{1,0:T(8,128)(2,1)S(1)} %convolution_convert_fusion) | copy-start | bytes 22020100
  118.9 60.2 %collective-permute-start = (bf16[1792,1024]{1,0:T(8,128)(2,1)}, bf16[1792,1024]{1,0:T(8,128)(2,1)}, u32[]{:S(2)}, u32[]{:S(2)}) collective-permute-start(bf16[1792,1024]{1,0:T(8,128)(2,1)} %dynamic-slice_bitcast_fusion), channel_id=1, source_target_pairs={{0,1},{1,0},{2,3},{3,2},{4,5},{5,4},{6,7},{7,6},{8,9},{9,8},{10,11... | collective-permute-start | bytes 11010056 | tf_op jit(solution)/shard_map/ppermute | solution.py:48
  171.5 145.0 %all-to-all-start.1 = ((bf16[4,320,896]{2,1,0:T(8,128)(2,1)}), bf16[4,320,896]{2,1,0:T(8,128)(2,1)S(1)}, u32[]{:S(2)}, u32[]{:S(2)}) async-start(bf16[4,320,896]{2,1,0:T(8,128)(2,1)} %pad_maximum_fusion.2), calls=%async_computation.1 | async-start | bytes 4587520 | tf_op jit(solution)/shard_map/all_to_all | solution.py:89
  179.1 196.7 %reduce-scatter.2.cloned.1.call-start = ((), (), s32[]{:S(2)}) async-start(), calls=%async_computation.5 | async-start | bytes 4587520 | tf_op jit(solution)/shard_map/reduce_scatter | solution.py:104
  186.0 130.6 %slice-start = ((bf16[320,4608]{1,0:T(8,128)(2,1)}), bf16[320,1024]{1,0:T(8,128)(2,1)S(1)}, s32[]{:S(2)}) async-start(bf16[320,4608]{1,0:T(8,128)(2,1)} %all_to_all.19), calls=%async_computation.6 | async-start | bytes 1310720 | tf_op jit(solution)/shard_map/split | solution.py:15
  371.9 3.8 %copy-start.1 = (bf16[128,3584]{1,0:T(8,128)(2,1)S(1)}, bf16[128,3584]{1,0:T(8,128)(2,1)}, u32[]{:S(2)}) copy-start(bf16[128,3584]{1,0:T(8,128)(2,1)} %param.9) | copy-start | bytes 2752516
Sparse Core Ops, SparseCore 0:
  186.2 157.8 reduce-scatter.1
